TPU v7x, 32 devices: a whole 2x2x4 slice. The times are simulated.
32 devices in a mesh: dom: 8 (over z, x), sub: 4 (over y, core).
Axes of the slice: x: 2, y: 2, z: 4, core: 2. Of those that a mesh axis runs over, the one named last changes fastest.
Arguments:
- primitive: float32 [5, 65536], P(None, ('dom', 'sub')), may hold values from -3 to 3
- gradient: float32 [15, 65536], P(None, ('dom', 'sub')), may hold values from -1.5 to 1.5
- volume: float32 [65536], P(('dom', 'sub')), may hold values from 0.5 to 4
- face_left: int32 [196608], P(('dom', 'sub')), may hold values from 0 to 2047
- face_right: int32 [196608], P(('dom', 'sub')), may hold values from 0 to 4095, as said below
- face_angles: float32 [2, 196608], P(None, ('dom', 'sub')), may hold values from -3.140625 to 3.140625
- face_area: float32 [196608], P(('dom', 'sub')), may hold values from 0.2 to 2
- face_offsets: float32 [6, 196608], P(None, ('dom', 'sub')), may hold values from -1 to 1
- rim_left: int32 [16384], P(('dom', 'sub')), may hold values from 0 to 511
- rim_right: int32 [16384], P(('dom', 'sub')), may hold values from 0 to 511
- rim_angles: float32 [2, 16384], P(None, ('dom', 'sub')), may hold values from -3.140625 to 3.140625
- rim_area: float32 [16384], P(('dom', 'sub')), may hold values from 0.2 to 2
- rim_offsets: float32 [6, 16384], P(None, ('dom', 'sub')), may hold values from -1 to 1
- send_list: int32 [512], P(('dom', 'sub')), may hold values from -1 to 15, as said below
Outputs:
- change_rate: float32 [5, 65536], P(None, ('dom', 'sub'))
- new_conserved: float32 [5, 65536], P(None, ('dom', 'sub'))
- time_step: float32 [], replicated
Inputs may be any that keep to these rules, and one draw needn't show every extreme that they name: `send_list`: an entry is a block number of the sending device or -1 for an unused slot; for each peer the used slots come first, at most 4 of them, a device sends no block to itself, and each device fills all 4 slots of one peer. `face_right`: an entry of at least 2048 names ghost cell (s * 4 + j) * 128 + k only where slot j of the sending peer s is used.
All inputs are finite; a program needn't handle non-finite values.
Results may differ from a plain program's by a relative error of at most 0.0003.
Values sent between devices are 32-bit elements; how exact they have to be, the bound alone decides.
A program may use at most 64 MiB of HBM per device.

v0:
```python
import jax
import jax.numpy as jnp
from jax import lax
from jax.sharding import PartitionSpec as P

BLK = 128
RIM = 4


adiabatic = 5.0 / 3.0
courant = 0.3


def shifted(value, axis, steps):
    count = lax.axis_size(axis)
    first, last = (max(0, -steps), min(count, count - steps))
    return lax.ppermute(value, axis, [(source, source + steps) for source in range(first, last)])


def face_states(side_cells, shifts):
    centre_values = side_cells[:5]
    slopes = side_cells[5:].reshape(5, 3, -1)
    values = centre_values + jnp.sum(slopes * shifts[None], axis=1)
    return (jnp.exp(values[0]), values[1:4], jnp.exp(values[4]))


def conserved_flux(density, velocity, pressure, normal):
    normal_speed = jnp.sum(velocity * normal, axis=0)
    energy = pressure / (adiabatic - 1.0) + 0.5 * density * jnp.sum(velocity * velocity, axis=0)
    conserved = jnp.concatenate([density[None], density * velocity, energy[None]], 0)
    flux_vector = jnp.concatenate(
        [
            (density * normal_speed)[None],
            density * velocity * normal_speed + pressure * normal,
            ((energy + pressure) * normal_speed)[None],
        ],
        0,
    )
    return (normal_speed, energy, conserved, flux_vector)


def star_flux(
    density,
    velocity,
    pressure,
    normal,
    normal_speed,
    energy,
    conserved,
    flux_vector,
    signal,
    contact,
):
    mass_rate = density * (signal - normal_speed)
    factor = mass_rate / (signal - contact)
    star_state = factor * jnp.concatenate(
        [
            jnp.ones_like(density)[None],
            velocity + (contact - normal_speed) * normal,
            (energy / density + (contact - normal_speed) * (contact + pressure / mass_rate))[None],
        ],
        0,
    )
    return flux_vector + signal * (star_state - conserved)


def hllc_flux(left_cells, right_cells, angles, offsets):
    normal = jnp.stack(
        [
            jnp.sin(angles[0]) * jnp.cos(angles[1]),
            jnp.sin(angles[0]) * jnp.sin(angles[1]),
            jnp.cos(angles[0]),
        ],
        0,
    )
    density_left, velocity_left, pressure_left = face_states(left_cells, offsets[0:3])
    density_right, velocity_right, pressure_right = face_states(right_cells, offsets[3:6])
    speed_left, energy_left, state_left, flux_left = conserved_flux(
        density_left, velocity_left, pressure_left, normal
    )
    speed_right, energy_right, state_right, flux_right = conserved_flux(
        density_right, velocity_right, pressure_right, normal
    )
    sound_left = jnp.sqrt(adiabatic * pressure_left / density_left)
    sound_right = jnp.sqrt(adiabatic * pressure_right / density_right)
    signal_left = jnp.minimum(speed_left - sound_left, speed_right - sound_right)
    signal_right = jnp.maximum(speed_left + sound_left, speed_right + sound_right)
    mass_left = density_left * (signal_left - speed_left)
    mass_right = density_right * (signal_right - speed_right)
    contact = (
        pressure_right - pressure_left + mass_left * speed_left - mass_right * speed_right
    ) / (mass_left - mass_right)
    star_left = star_flux(
        density_left,
        velocity_left,
        pressure_left,
        normal,
        speed_left,
        energy_left,
        state_left,
        flux_left,
        signal_left,
        contact,
    )
    star_right = star_flux(
        density_right,
        velocity_right,
        pressure_right,
        normal,
        speed_right,
        energy_right,
        state_right,
        flux_right,
        signal_right,
        contact,
    )
    return jnp.where(
        signal_left >= 0,
        flux_left,
        jnp.where(contact >= 0, star_left, jnp.where(signal_right > 0, star_right, flux_right)),
    )


def cell_conserved(primitive):
    density = jnp.exp(primitive[0])
    pressure = jnp.exp(primitive[4])
    velocity = primitive[1:4]
    energy = pressure / (adiabatic - 1.0) + 0.5 * density * jnp.sum(velocity * velocity, axis=0)
    return jnp.concatenate([density[None], density * velocity, energy[None]], 0)


def signal_limit(primitive, volume):
    density = jnp.exp(primitive[0])
    pressure = jnp.exp(primitive[4])
    velocity = primitive[1:4]
    sound_speed = jnp.sqrt(adiabatic * pressure / density)
    flow_speed = jnp.sqrt(jnp.sum(velocity * velocity, axis=0))
    return volume ** (1.0 / 3.0) / (sound_speed + flow_speed)


def body(
    primitive,
    gradient,
    volume,
    face_left,
    face_right,
    face_angles,
    face_area,
    face_offsets,
    rim_left,
    rim_right,
    rim_angles,
    rim_area,
    rim_offsets,
    send_list,
):
    local_cells = primitive.shape[1]
    block_count = local_cells // BLK
    peer_count = lax.axis_size("sub")
    capacity = send_list.shape[0] // peer_count
    rim_width = RIM * BLK
    position = lax.axis_index("dom")
    dom_count = lax.axis_size("dom")
    packed = jnp.concatenate([primitive, gradient], 0)
    blocks = packed.reshape(20, block_count, BLK)
    wanted = send_list.reshape(peer_count, capacity)
    picked = jnp.take(blocks, jnp.maximum(wanted, 0).reshape(-1), axis=1)
    picked = picked * (wanted.reshape(-1) >= 0).astype(jnp.float32)[None, :, None]
    outgoing = picked.reshape(20, peer_count, capacity * BLK)
    arrived = lax.all_to_all(outgoing, "sub", split_axis=1, concat_axis=1, tiled=True)
    ghosts = arrived.reshape(20, peer_count * capacity * BLK)
    combined = jnp.concatenate([packed, ghosts], 1)
    weighted = (
        hllc_flux(
            jnp.take(packed, face_left, axis=1),
            jnp.take(combined, face_right, axis=1),
            face_angles,
            face_offsets,
        )
        * face_area
    )
    totals = (
        jnp.zeros((5, combined.shape[1]), jnp.float32)
        .at[:, face_left]
        .add(weighted)
        .at[:, face_right]
        .add(-weighted)
    )
    net_flux = totals[:, :local_cells]
    ghost_back = totals[:, local_cells:].reshape(5, peer_count, capacity * BLK)
    returned = lax.all_to_all(ghost_back, "sub", split_axis=1, concat_axis=1, tiled=True)
    slot_target = jnp.where(wanted < 0, block_count, wanted).reshape(-1)
    net_flux = (
        net_flux.reshape(5, block_count, BLK)
        .at[:, slot_target]
        .add(returned.reshape(5, peer_count * capacity, BLK), mode="drop")
        .reshape(5, local_cells)
    )
    tail_cells = packed[:, local_cells - rim_width :]
    head_cells = packed[:, :rim_width]
    rim_mask = (position < dom_count - 1).astype(jnp.float32)
    following = shifted(head_cells, "dom", -1)
    rim_flux = hllc_flux(
        jnp.take(tail_cells, rim_left, axis=1),
        jnp.take(following, rim_right, axis=1),
        rim_angles,
        rim_offsets,
    ) * (rim_area * rim_mask)
    net_flux = net_flux.at[:, local_cells - rim_width + rim_left].add(rim_flux)
    rim_back = jnp.zeros((5, rim_width), jnp.float32).at[:, rim_right].add(-rim_flux)
    inflow = shifted(rim_back, "dom", 1)
    net_flux = net_flux.at[:, :rim_width].add(inflow)
    local_limit = jnp.min(signal_limit(primitive, volume))
    smallest = lax.pmin(local_limit, ("dom", "sub"))
    time_step = courant * smallest
    change_rate = -net_flux / volume
    new_conserved = cell_conserved(primitive) + time_step * change_rate
    return (change_rate, new_conserved, time_step)


def solution(mesh):
    in_specs = (
        P(None, ("dom", "sub")),
        P(None, ("dom", "sub")),
        P(("dom", "sub")),
        P(("dom", "sub")),
        P(("dom", "sub")),
        P(None, ("dom", "sub")),
        P(("dom", "sub")),
        P(None, ("dom", "sub")),
        P(("dom", "sub")),
        P(("dom", "sub")),
        P(None, ("dom", "sub")),
        P(("dom", "sub")),
        P(None, ("dom", "sub")),
        P(("dom", "sub")),
    )
    out_specs = (P(None, ("dom", "sub")), P(None, ("dom", "sub")), P())
    return jax.shard_map(body, mesh=mesh, in_specs=in_specs, out_specs=out_specs, check_vma=False)
```

profile of v0, /device:TPU:0, one launch (start us, length us, event | category | flops | bytes accessed | tf_op | source)
XLA Modules:
  0.0 219.5 jit_solution(2858463230925857631)
XLA Ops:
  0.7 1.0 pad_maximum_fusion.1
  1.7 0.4 copy.426
  2.1 0.8 fusion.36
  2.8 1.3 collective-permute-start
  4.1 1.2 compare_select_fusion.6
  5.3 0.7 broadcast_compare_fusion.4
  6.1 0.6 gather_fusion.1
  6.8 0.1 reshape.195
  6.9 0.1 broadcast_in_dim.91
  7.2 0.7 copy.430
  7.9 4.3 %all-to-all-start = ((f32[20,4,512]{2,0,1:T(8,128)}), f32[20,4,512]{2,0,1:T(8,128)S(1)}, u32[]{:S(2)}, u32[]{:S(2)}) async-start(f32[20,4,512]{2,0,1:T(8,128)} %copy.430), calls=%async_computation | async-start | bytes 393216 | tf_op jit(solution)/shard_map/all_to_all | solution.py:170
  12.2 0.6 compare_select_fusion.4
  12.8 0.6 compare_select_fusion.2
  13.4 0.6 compare_and_fusion
  14.0 0.6 fusion.13
  14.7 1.0 gather_fusion.3
  15.8 0.1 copy.441
  15.9 0.1 cosine_multiply_fusion.1
  16.0 20.9 %gather_fusion = f32[6144,20]{1,0:T(8,128)} fusion(f32[20,2048]{0,1:T(8,128)S(1)} %copy.426, s32[6144]{0:T(1024)S(1)} %get-tuple-element.113), kind=kCustom, calls=%fused_computation.2 | custom fusion | bytes 1007616 | tf_op jit(solution)/shard_map/jit(_take)/gather | solution.py:175
  36.9 2.4 %copy.427 = f32[6144,20]{0,1:T(8,128)S(1)} copy(f32[6144,20]{1,0:T(8,128)} %gather_fusion) | data formatting | bytes 983040 | tf_op jit(solution)/shard_map/jit(_take)/gather | solution.py:175
  39.4 0.7 fusion.37
  40.1 1.4 cosine_multiply_fusion
  41.5 0.6 fusion.23
  42.3 0.6 fusion.22
  43.0 0.2 reshape.185
  43.2 1.0 gather_fusion.4
  44.3 0.1 copy.443
  44.8 0.7 negate_bitcast_fusion.1
  45.5 0.1 copy.446
  45.7 2.9 %scatter_custom_fusion.4 = f32[5,512]{0,1:T(8,128)} fusion(s32[512]{0:T(512)S(1)} %compare_select_fusion.3, f32[512,5]{1,0:T(8,128)S(1)} %copy.446, f32[]{:T(128)} %constant.115.clone.1), kind=kCustom, calls=%fused_computation.38 | custom fusion | flops 2560 | bytes 10244 | tf_op jit(solution)/shard_map/scatter-add | solution.py:210
  48.6 5.3 %collective-permute-start.1 = (f32[5,512]{0,1:T(8,128)}, f32[5,512]{0,1:T(8,128)}, u32[]{:S(2)}, u32[]{:S(2)}) collective-permute-start(f32[5,512]{0,1:T(8,128)} %scatter_custom_fusion.4), channel_id=1, source_target_pairs={{0,4},{4,8},{8,12},{12,16},{16,20},{20,24},{24,28},{1,5},{5,9},{9,... | collective-permute-start | bytes 30728 | tf_op jit(solution)/shard_map/ppermute | solution.py:17
  53.9 0.1 copy.431
  54.2 0.8 pad_maximum_fusion
  54.9 1.6 copy.432
  56.6 20.9 %gather_fusion.2 = f32[6144,20]{1,0:T(8,128)} fusion(f32[20,4096]{0,1:T(8,128)S(1)} %copy.432, s32[6144]{0:T(1024)S(1)} %copy-done.6), kind=kCustom, calls=%fused_computation.4 | custom fusion | bytes 1007616 | tf_op jit(solution)/shard_map/jit(_take)/gather | solution.py:176
  77.5 2.4 %copy.433 = f32[6144,20]{0,1:T(8,128)S(1)} copy(f32[6144,20]{1,0:T(8,128)} %gather_fusion.2) | data formatting | bytes 983040 | tf_op jit(solution)/shard_map/jit(_take)/gather | solution.py:176
  80.0 0.2 reshape.188
  80.2 0.7 multiply_reduce_fusion
  80.9 0.3 multiply_reduce_fusion.2
  81.3 0.4 subtract_divide_fusion.1
  81.7 0.3 multiply_add_fusion.7
  82.0 0.1 broadcast_multiply_fusion
  82.1 0.1 multiply_add_fusion.4
  82.3 0.1 multiply_add_fusion.2
  82.5 0.5 negate_bitcast_fusion
  83.0 2.2 %copy.434 = f32[6144,5]{1,0:T(8,128)} copy(f32[6144,5]{0,1:T(8,128)S(1)} %bitcast.83) | data formatting | bytes 245760 | tf_op jit(solution)/shard_map/mul | solution.py:174
  85.2 2.2 %copy.435 = f32[6144,5]{1,0:T(8,128)} copy(f32[6144,5]{0,1:T(8,128)S(1)} %get-tuple-element.61) | data formatting | bytes 245760 | tf_op jit(solution)/shard_map/neg | solution.py:187
  87.5 34.0 %scatter_custom_fusion = f32[5,4096]{0,1:T(8,128)S(1)} fusion(s32[6144]{0:T(1024)} %get-tuple-element.114, f32[6144,5]{1,0:T(8,128)} %copy.434, f32[]{:T(128)} %constant.115.clone.1), kind=kCustom, calls=%fused_computation.12 | custom fusion | flops 30720 | bytes 82432 | tf_op jit(solution)/shard_map/scatter-add | solution.py:185
  121.5 34.3 %scatter_fusion = f32[5,4096]{0,1:T(8,128)S(1)} fusion(f32[5,4096]{0,1:T(8,128)S(1)} %scatter_custom_fusion, s32[6144]{0:T(1024)S(1)} %copy-done.5, f32[6144,5]{1,0:T(8,128)} %copy.435), kind=kCustom, calls=%fused_computation.6 | custom fusion | flops 30720 | bytes 393216 | tf_op jit(solution)/shard_map/scatter-add | solution.py:187
  155.8 1.1 fusion.35
  156.9 2.2 %copy.436 = f32[5,4,512]{2,0,1:T(8,128)} copy(f32[5,4,512]{0,2,1:T(8,128)} %bitcast.75) | data formatting | bytes 81920 | tf_op jit(solution)/shard_map/reshape | solution.py:190
  159.1 3.3 %all-to-all-start.1 = ((f32[5,4,512]{2,0,1:T(8,128)}), f32[5,4,512]{2,0,1:T(8,128)S(1)}, u32[]{:S(2)}, u32[]{:S(2)}) async-start(f32[5,4,512]{2,0,1:T(8,128)} %copy.436), calls=%async_computation.1 | async-start | bytes 131072 | tf_op jit(solution)/shard_map/all_to_all | solution.py:191
  162.4 42.1 %pmin.7 = f32[]{:T(128)} all-reduce(f32[]{:T(128)} %fusion.22), channel_id=1, replica_groups=mesh['dom'=8,'sub'=4] {'dom','sub'}, use_global_device_ids=true, to_apply=%region_20.22 | all-reduce | flops 1 | bytes 8 | tf_op jit(solution)/shard_map/pmin | solution.py:214
  204.6 0.4 copy.447
  205.6 0.6 compare_reduce_fusion
  206.2 0.1 copy.445
  206.4 0.3 copy.438
  206.8 1.1 scatter_fusion.1
  207.9 0.4 copy.444
  208.3 3.9 %scatter_fusion.2 = f32[5,2048]{0,1:T(8,128)S(1)} fusion(f32[5,2048]{0,1:T(8,128)S(1)} %copy.444, s32[512]{0:T(512)S(1)} %copy-done.17, f32[512,5]{1,0:T(8,128)S(1)} %copy.445), kind=kCustom, calls=%fused_computation.8 | custom fusion | flops 2560 | bytes 32768 | tf_op jit(solution)/shard_map/scatter-add | solution.py:209
  212.2 1.7 fusion.2
  213.9 1.3 multiply_add_fusion
  215.3 2.2 copy.448
  217.5 1.0 copy.449
  (107 shorter events, 1.6 us)
Async XLA Ops:
  0.6 14.0 %copy-start = (f32[5,2048]{1,0:T(8,128)S(1)}, f32[5,2048]{1,0:T(8,128)}, u32[]{:S(2)}) copy-start(f32[5,2048]{1,0:T(8,128)} %param.18) | copy-start | bytes 122884
  0.6 11.5 %copy-start.19 = (s32[512]{0:T(512)S(1)}, s32[512]{0:T(512)}, u32[]{:S(2)}) copy-start(s32[512]{0:T(512)} %param.27) | copy-start | bytes 6148
  0.7 11.5 %copy-start.18 = (s32[512]{0:T(512)S(1)}, s32[512]{0:T(512)}, u32[]{:S(2)}) copy-start(s32[512]{0:T(512)} %param.26) | copy-start | bytes 6148
  0.7 12.1 %copy-start.7 = (s32[6144]{0:T(1024)S(1)}, s32[6144]{0:T(1024)}, u32[]{:S(2)}) copy-start(s32[6144]{0:T(1024)} %param.22) | copy-start | bytes 73732
  0.7 13.3 %copy-start.8 = (s32[6144]{0:T(1024)S(1)}, s32[6144]{0:T(1024)}, u32[]{:S(2)}) copy-start(s32[6144]{0:T(1024)} %param.21) | copy-start | bytes 73732
  1.7 14.2 %copy-start.16 = (f32[6,512]{1,0:T(8,128)S(1)}, f32[6,512]{1,0:T(8,128)}, u32[]{:S(2)}) copy-start(f32[6,512]{1,0:T(8,128)} %param.30) | copy-start | bytes 36868
  1.7 14.2 %copy-start.20 = (f32[2,512]{1,0:T(2,128)S(1)}, f32[2,512]{1,0:T(2,128)}, u32[]{:S(2)}) copy-start(f32[2,512]{1,0:T(2,128)} %param.28) | copy-start | bytes 12292
  2.8 40.4 %collective-permute-start = (f32[20,512]{0,1:T(8,128)}, f32[20,512]{0,1:T(8,128)S(1)}, u32[]{:S(2)}, u32[]{:S(2)}) collective-permute-start(f32[20,512]{0,1:T(8,128)} %get-tuple-element.80), channel_id=1, source_target_pairs={{4,0},{8,4},{12,8},{16,12},{20,16},{24,20},{28,24},{5,1},{9,5},{13... | collective-permute-start | bytes 122888 | tf_op jit(solution)/shard_map/ppermute | solution.py:17
  7.9 46.0 %all-to-all-start = ((f32[20,4,512]{2,0,1:T(8,128)}), f32[20,4,512]{2,0,1:T(8,128)S(1)}, u32[]{:S(2)}, u32[]{:S(2)}) async-start(f32[20,4,512]{2,0,1:T(8,128)} %copy.430), calls=%async_computation | async-start | bytes 393216 | tf_op jit(solution)/shard_map/all_to_all | solution.py:170
  36.9 2.4 %copy-start.4 = (f32[6,6144]{1,0:T(8,128)S(1)}, f32[6,6144]{1,0:T(8,128)}, u32[]{:S(2)}) copy-start(f32[6,6144]{1,0:T(8,128)} %param.25) | copy-start | bytes 442372
  36.9 3.2 %copy-start.10 = (f32[2,6144]{1,0:T(2,128)S(1)}, f32[2,6144]{1,0:T(2,128)}, u32[]{:S(2)}) copy-start(f32[2,6144]{1,0:T(2,128)} %param.23) | copy-start | bytes 147460
  36.9 5.3 %copy-start.23 = (f32[512]{0:T(512)S(1)}, f32[512]{0:T(512)}, u32[]{:S(2)}) copy-start(f32[512]{0:T(512)} %param.29) | copy-start | bytes 6148
  36.9 5.4 %copy-start.11 = (f32[2048]{0:T(1024)S(1)}, f32[2048]{0:T(1024)}, u32[]{:S(2)}) copy-start(f32[2048]{0:T(1024)} %param.20) | copy-start | bytes 24580
  42.2 11.9 %copy-start.1 = (f32[15,2048]{1,0:T(8,128)S(1)}, f32[15,2048]{1,0:T(8,128)}, u32[]{:S(2)}) copy-start(f32[15,2048]{1,0:T(8,128)} %param.19) | copy-start | bytes 368644
  43.2 10.9 %copy-start.21 = (f32[5]{0:T(128)}, f32[5]{0:T(128)S(1)}, u32[]{:S(2)}) copy-start(f32[5]{0:T(128)S(1)} %pad.38.clone) | copy-start | bytes 64
  44.3 12.3 %copy-start.6 = (s32[6144]{0:T(1024)S(1)}, s32[6144]{0:T(1024)}, u32[]{:S(2)}) copy-start(s32[6144]{0:T(1024)} %get-tuple-element.112) | copy-start | bytes 73732
  48.6 163.6 %collective-permute-start.1 = (f32[5,512]{0,1:T(8,128)}, f32[5,512]{0,1:T(8,128)}, u32[]{:S(2)}, u32[]{:S(2)}) collective-permute-start(f32[5,512]{0,1:T(8,128)} %scatter_custom_fusion.4), channel_id=1, source_target_pairs={{0,4},{4,8},{8,12},{12,16},{16,20},{20,24},{24,28},{1,5},{5,9},{9,... | collective-permute-start | bytes 30728 | tf_op jit(solution)/shard_map/ppermute | solution.py:17
  77.5 2.4 %copy-start.14 = (pred[6144]{0:T(1024)(128)(4,1)S(1)}, pred[6144]{0:T(1024)(128)(4,1)}, u32[]{:S(2)}) copy-start(pred[6144]{0:T(1024)(128)(4,1)} %compare_and_fusion) | copy-start | bytes 18436
  77.5 2.7 %copy-start.2 = (f32[3,6144]{1,0:T(4,128)S(1)}, f32[3,6144]{1,0:T(4,128)}, u32[]{:S(2)}) copy-start(f32[3,6144]{1,0:T(4,128)} %get-tuple-element.94) | copy-start | bytes 221188
  77.5 2.7 %copy-start.3 = (f32[3,6144]{1,0:T(4,128)S(1)}, f32[3,6144]{1,0:T(4,128)}, u32[]{:S(2)}) copy-start(f32[3,6144]{1,0:T(4,128)} %get-tuple-element.95) | copy-start | bytes 221188
  80.0 2.5 %copy-start.15 = (f32[6144]{0:T(1024)S(1)}, f32[6144]{0:T(1024)}, u32[]{:S(2)}) copy-start(f32[6144]{0:T(1024)} %param.24) | copy-start | bytes 73732
  80.0 2.5 %copy-start.22 = (f32[5]{0:T(128)S(1)}, f32[5]{0:T(128)}, u32[]{:S(2)}) copy-start(f32[5]{0:T(128)} %copy-done.21) | copy-start | bytes 64
  85.2 36.2 %copy-start.5 = (s32[6144]{0:T(1024)S(1)}, s32[6144]{0:T(1024)}, u32[]{:S(2)}) copy-start(s32[6144]{0:T(1024)} %get-tuple-element.111) | copy-start | bytes 73732
  155.7 6.7 %copy-start.13 = (f32[1,2048]{1,0:T(1,128)S(1)}, f32[1,2048]{1,0:T(1,128)}, u32[]{:S(2)}) copy-start(f32[1,2048]{1,0:T(1,128)} %get-tuple-element.103) | copy-start | bytes 24580
  155.8 50.5 %copy-start.9 = (f32[5,512]{1,0:T(8,128)S(1)}, f32[5,512]{1,0:T(8,128)}, u32[]{:S(2)}) copy-start(f32[5,512]{1,0:T(8,128)} %get-tuple-element.45) | copy-start | bytes 30724
  155.8 51.0 %copy-start.24 = (s32[16]{0:T(128)S(1)}, s32[16]{0:T(128)}, u32[]{:S(2)}) copy-start(s32[16]{0:T(128)} %get-tuple-element.143) | copy-start | bytes 196
  156.9 51.4 %copy-start.17 = (s32[512]{0:T(512)S(1)}, s32[512]{0:T(512)}, u32[]{:S(2)}) copy-start(s32[512]{0:T(512)} %get-tuple-element.142) | copy-start | bytes 6148
  156.9 57.0 %copy-start.12 = (f32[2048]{0:T(1024)S(1)}, f32[2048]{0:T(1024)}, u32[]{:S(2)}) copy-start(f32[2048]{0:T(1024)} %param.20) | copy-start | bytes 24580
  159.1 47.6 %all-to-all-start.1 = ((f32[5,4,512]{2,0,1:T(8,128)}), f32[5,4,512]{2,0,1:T(8,128)S(1)}, u32[]{:S(2)}, u32[]{:S(2)}) async-start(f32[5,4,512]{2,0,1:T(8,128)} %copy.436), calls=%async_computation.1 | async-start | bytes 131072 | tf_op jit(solution)/shard_map/all_to_all | solution.py:191
where the time goes:
time: 220 us
  other arithmetic  92.7 us (42%)
  local copies, waits for them, and re-layouts  67.3 us (31%)
  blocking collectives  42.1 us (19%)
  starting transfers between devices  14.2 us (6%)
  between operations  3.26 us (1%)
    scatter-add x2, other arithmetic, body(): totals = jnp.zeros((5, combined.shape[1]), jnp.float32).at[:, face_left]....  68.2 us
    pmin x1, blocking collectives, body(): smallest = lax.pmin(local_limit, ('dom', 'sub'))  42.1 us
    gather x2, local copies, waits for them, and re-layouts, body(): jnp.take(packed, face_left, axis=1)  23.3 us
    gather x2, local copies, waits for them, and re-layouts, body(): jnp.take(combined, face_right, axis=1)  23.3 us
    ppermute x2, starting transfers between devices, shifted(): lax.ppermute(value, axis, [(source, source + steps) for source in range(f...  6.6 us
  transfers between devices with their start and end apart: 4, of which 0 were waited for; matrix products, arithmetic and copies ran while one was open for 69% of the time, Pallas kernels for 0%

commit v1 on v0

v1 whole, which is shorter than its diff:
```python
import functools
import jax
import jax.numpy as jnp
from jax import lax
from jax.experimental import pallas as pl
from jax.experimental.pallas import tpu as pltpu
from jax.sharding import PartitionSpec as P

BLK = 128
RIM = 4
GROUP = 4
PIECES = 2

adiabatic = 5.0 / 3.0
courant = 0.3
MESH = pl.DeviceIdType.MESH


def side_state(q, offsets):
    def value(c):
        slopes = q(5 + 3 * c) * offsets[0] + q(6 + 3 * c) * offsets[1] + q(7 + 3 * c) * offsets[2]
        return q(c) + slopes

    return jnp.exp(value(0)), [value(1), value(2), value(3)], jnp.exp(value(4))


def conserved_flux(density, velocity, pressure, normal):
    speed = velocity[0] * normal[0] + velocity[1] * normal[1] + velocity[2] * normal[2]
    square = velocity[0] * velocity[0] + velocity[1] * velocity[1] + velocity[2] * velocity[2]
    energy = pressure / (adiabatic - 1.0) + 0.5 * density * square
    momentum = [density * v for v in velocity]
    conserved = [density] + momentum + [energy]
    flux = (
        [density * speed]
        + [m * speed + pressure * n for m, n in zip(momentum, normal)]
        + [(energy + pressure) * speed]
    )
    return speed, energy, conserved, flux


def star_flux(density, velocity, pressure, normal, speed, energy, conserved, flux, signal, contact, mass_rate):
    factor = mass_rate / (signal - contact)
    jump = contact - speed
    star = (
        [factor]
        + [factor * (v + jump * n) for v, n in zip(velocity, normal)]
        + [factor * (energy / density + jump * (contact + pressure / mass_rate))]
    )
    return [f + signal * (s - u) for f, s, u in zip(flux, star, conserved)]


def hllc(left, right, angles, offsets):
    sin_a = jnp.sin(angles[0])
    normal = [sin_a * jnp.cos(angles[1]), sin_a * jnp.sin(angles[1]), jnp.cos(angles[0])]
    dl, vl, pl_ = side_state(left, offsets[:3])
    dr, vr, pr = side_state(right, offsets[3:])
    ul, el, cl, fl = conserved_flux(dl, vl, pl_, normal)
    ur, er, cr, fr = conserved_flux(dr, vr, pr, normal)
    sound_l = jnp.sqrt(adiabatic * pl_ / dl)
    sound_r = jnp.sqrt(adiabatic * pr / dr)
    signal_l = jnp.minimum(ul - sound_l, ur - sound_r)
    signal_r = jnp.maximum(ul + sound_l, ur + sound_r)
    mass_l = dl * (signal_l - ul)
    mass_r = dr * (signal_r - ur)
    contact = (pr - pl_ + mass_l * ul - mass_r * ur) / (mass_l - mass_r)
    star_l = star_flux(dl, vl, pl_, normal, ul, el, cl, fl, signal_l, contact, mass_l)
    star_r = star_flux(dr, vr, pr, normal, ur, er, cr, fr, signal_r, contact, mass_r)
    out = []
    for a, b, c, d in zip(fl, star_l, star_r, fr):
        inner = jnp.where(contact >= 0, b, jnp.where(signal_r > 0, c, d))
        out.append(jnp.where(signal_l >= 0, a, inner))
    return out


def lane_gather(row, index):
    table = jnp.broadcast_to(row, index.shape)
    return jnp.take_along_axis(table, index, axis=1, mode="promise_in_bounds")


def kernel(
    dims,
    send_list,
    prim,
    grad,
    volume,
    face_left,
    face_right,
    face_angles,
    face_area,
    face_offsets,
    rim_left,
    rim_right,
    rim_angles,
    rim_area,
    rim_offsets,
    rate_out,
    new_out,
    step_out,
    outgoing,
    ghosts,
    following,
    table,
    min_own,
    min_sub,
    min_group,
    min_dom,
    gback_send,
    gback_recv,
    rback_send,
    rback_recv,
    cells,
    hi_left,
    lo_left,
    hi_right,
    lo_right,
    angles,
    offsets,
    area,
    gathered_l,
    gathered_r,
    pieces,
    ghost_send_sem,
    ghost_recv_sem,
    rim_send_sem,
    rim_recv_sem,
    min_send_sem,
    min_recv_sem,
    dmin_send_sem,
    dmin_recv_sem,
    gback_send_sem,
    gback_recv_sem,
    rback_send_sem,
    rback_recv_sem,
):
    n_dom, n_sub, capacity, blocks, face_rows = dims
    rows = face_rows + RIM
    ghost_blocks = n_sub * capacity
    me_dom = lax.axis_index("dom")
    me_sub = lax.axis_index("sub")
    before = lax.rem(me_dom + n_dom - 1, n_dom)
    after = lax.rem(me_dom + 1, n_dom)

    def sub_peer(off):
        return lax.rem(me_sub + off, n_sub)

    def dom_peer(off):
        return lax.rem(me_dom + off, n_dom)

    barrier = pltpu.get_barrier_semaphore()
    for off in range(1, n_sub):
        pl.semaphore_signal(barrier, inc=1, device_id=(me_dom, sub_peer(off)), device_id_type=MESH)
    for off in range(1, n_dom):
        pl.semaphore_signal(barrier, inc=1, device_id=(dom_peer(off), me_sub), device_id_type=MESH)

    for h in range(blocks):
        table[h, 0:5, :] = prim[:, h * BLK : (h + 1) * BLK]
        table[h, 5:8, :] = jnp.zeros((3, BLK), jnp.float32)
        table[h, 8:23, :] = grad[:, h * BLK : (h + 1) * BLK]
        table[h, 23:24, :] = jnp.zeros((1, BLK), jnp.float32)

    for off in range(1, n_sub):
        for j in range(capacity):
            block = jnp.maximum(send_list[sub_peer(off) * capacity + j], 0)
            outgoing[off, j] = table[block]

    for r in range(5):
        for h in range(blocks):
            cells[r, h : h + 1, :] = prim[r : r + 1, h * BLK : (h + 1) * BLK]
    density = jnp.exp(cells[0])
    pressure = jnp.exp(cells[4])
    square = cells[1] * cells[1] + cells[2] * cells[2] + cells[3] * cells[3]
    signal = jnp.sqrt(adiabatic * pressure / density) + jnp.sqrt(square)
    limit = jnp.exp(jnp.log(volume[...]) * (1.0 / 3.0)) / signal
    local_min = jnp.min(limit)
    min_own[...] = jnp.full(min_own.shape, local_min, jnp.float32)

    pl.semaphore_wait(barrier, n_sub - 1 + n_dom - 1)

    copies = []

    def ghost_copy(off):
        return pltpu.make_async_remote_copy(
            src_ref=outgoing.at[off],
            dst_ref=ghosts.at[off],
            send_sem=ghost_send_sem.at[off],
            recv_sem=ghost_recv_sem.at[off],
            device_id=(me_dom, sub_peer(off)),
            device_id_type=MESH,
        )

    ghost_copies = [ghost_copy(off) for off in range(1, n_sub)]
    for copy in ghost_copies:
        copy.start()
    rim_copy = pltpu.make_async_remote_copy(
        src_ref=table.at[0:RIM],
        dst_ref=following,
        send_sem=rim_send_sem,
        recv_sem=rim_recv_sem,
        device_id=(before, me_sub),
        device_id_type=MESH,
    )
    rim_copy.start()
    min_copies = [
        pltpu.make_async_remote_copy(
            src_ref=min_own,
            dst_ref=min_sub.at[off],
            send_sem=min_send_sem.at[off],
            recv_sem=min_recv_sem.at[off],
            device_id=(me_dom, sub_peer(off)),
            device_id_type=MESH,
        )
        for off in range(1, n_sub)
    ]
    for copy in min_copies:
        copy.start()

    hi_left[0:face_rows, :] = face_left[...] // BLK
    lo_left[0:face_rows, :] = lax.rem(face_left[...], BLK)
    hi_right[0:face_rows, :] = face_right[...] // BLK
    lo_right[0:face_rows, :] = lax.rem(face_right[...], BLK)
    area[0:face_rows, :] = face_area[...]
    twice = lambda ref: jnp.concatenate([ref[...], ref[...]], 0)
    hi_left[face_rows : face_rows + 8, :] = twice(rim_left) // BLK + (blocks - RIM)
    lo_left[face_rows : face_rows + 8, :] = lax.rem(twice(rim_left), BLK)
    hi_right[face_rows : face_rows + 8, :] = twice(rim_right) // BLK + (blocks + ghost_blocks)
    lo_right[face_rows : face_rows + 8, :] = lax.rem(twice(rim_right), BLK)
    last = me_dom == n_dom - 1
    area[face_rows : face_rows + 8, :] = twice(rim_area)
    for s in range(face_rows):
        for r in range(2):
            angles[r, s : s + 1, :] = face_angles[r : r + 1, s * BLK : (s + 1) * BLK]
        for r in range(6):
            offsets[r, s : s + 1, :] = face_offsets[r : r + 1, s * BLK : (s + 1) * BLK]
    for s in range(8):
        t = s % RIM
        for r in range(2):
            angles[r, face_rows + s : face_rows + s + 1, :] = rim_angles[r : r + 1, t * BLK : (t + 1) * BLK]
        for r in range(6):
            offsets[r, face_rows + s : face_rows + s + 1, :] = rim_offsets[r : r + 1, t * BLK : (t + 1) * BLK]

    main = pl.ds(0, face_rows)
    tail = pl.ds(face_rows, 8)

    def gather_local(count, place, shift):
        def step(r, carry):
            hl, ll, hr, lr = (ref[main, :] for ref in (hi_left, lo_left, hi_right, lo_right))
            left = jnp.zeros(hl.shape, jnp.float32)
            right = jnp.zeros(hl.shape, jnp.float32)
            for h in range(blocks):
                row = table[h, pl.ds(r + place, 1), :]
                left = jnp.where(hl == h, lane_gather(row, ll), left)
                right = jnp.where(hr == h, lane_gather(row, lr), right)
            gathered_l[r + shift, main, :] = left
            gathered_r[r + shift, main, :] = right
            hl, ll = hi_left[tail, :], lo_left[tail, :]
            left = jnp.zeros(hl.shape, jnp.float32)
            for h in range(blocks - RIM, blocks):
                row = table[h, pl.ds(r + place, 1), :]
                left = jnp.where(hl == h, lane_gather(row, ll), left)
            gathered_l[r + shift, tail, :] = left
            return carry

        lax.fori_loop(0, count, step, 0)

    gather_local(5, 0, 0)
    gather_local(15, 8, 5)

    for copy in min_copies:
        copy.wait()
    group_min = min_own[...]
    for off in range(1, n_sub):
        group_min = jnp.minimum(group_min, min_sub[off])
    min_group[...] = group_min

    rim_copy.wait()

    def gather_rim(count, place, shift):
        def step(r, carry):
            hr, lr = hi_right[tail, :], lo_right[tail, :]
            right = jnp.zeros(hr.shape, jnp.float32)
            for h in range(RIM):
                row = following[h, pl.ds(r + place, 1), :]
                right = jnp.where(hr == h + blocks + ghost_blocks, lane_gather(row, lr), right)
            gathered_r[r + shift, tail, :] = right
            return carry

        lax.fori_loop(0, count, step, 0)

    gather_rim(5, 0, 0)
    gather_rim(15, 8, 5)

    dmin_copies = [
        pltpu.make_async_remote_copy(
            src_ref=min_group,
            dst_ref=min_dom.at[off],
            send_sem=dmin_send_sem.at[off],
            recv_sem=dmin_recv_sem.at[off],
            device_id=(dom_peer(off), me_sub),
            device_id_type=MESH,
        )
        for off in range(1, n_dom)
    ]
    for copy in dmin_copies:
        copy.start()

    for copy in ghost_copies:
        copy.wait()

    def gather_ghosts(count, place, shift):
        def step(r, carry):
            hr, lr = hi_right[main, :], lo_right[main, :]
            right = gathered_r[r + shift, main, :]
            for off in range(1, n_sub):
                sender = lax.rem(me_sub + n_sub - off, n_sub)
                for j in range(capacity):
                    row = ghosts[off, j, pl.ds(r + place, 1), :]
                    right = jnp.where(hr == blocks + sender * capacity + j, lane_gather(row, lr), right)
            gathered_r[r + shift, main, :] = right
            return carry

        lax.fori_loop(0, count, step, 0)

    gather_ghosts(5, 0, 0)
    gather_ghosts(15, 8, 5)

    def flux_step(g, carry):
        here = pl.ds(pl.multiple_of(g * 8, 8), 8)
        flux = hllc(
            lambda c: gathered_l[c, here, :],
            lambda c: gathered_r[c, here, :],
            [angles[k, here, :] for k in range(2)],
            [offsets[k, here, :] for k in range(6)],
        )
        idle = jnp.logical_and(g * 8 >= face_rows, last)
        for c in range(5):
            value = jnp.where(idle, 0.0, flux[c] * area[here, :])
            big = value.astype(jnp.bfloat16).astype(jnp.float32)
            pieces[c, here, :] = big
            pieces[5 + c, here, :] = value - big
        return carry

    lax.fori_loop(0, (face_rows + 8) // 8, flux_step, 0)

    lane_iota = lax.broadcasted_iota(jnp.int32, (BLK, BLK), 0)

    def one_hot(lo, s):
        return jnp.where(lane_iota == lo[pl.ds(s, 1), :], 1.0, 0.0).astype(jnp.bfloat16)

    def spread(hi, s, first, count, sign):
        place = lax.broadcasted_iota(jnp.int32, (count, BLK), 0) + first
        match = place == hi[pl.ds(s, 1), :]
        parts = []
        for c in range(5 * PIECES):
            value = pieces[c, pl.ds(s, 1), :]
            value = value if sign > 0 else -value
            parts.append(jnp.where(match, value, 0.0))
        return jnp.concatenate(parts, 0).astype(jnp.bfloat16)

    def product(a, b):
        return lax.dot_general(a, b, (((1,), (1,)), ((), ())), preferred_element_type=jnp.float32)

    def fold(total, count):
        total = total.reshape(PIECES, 5, count, BLK)
        return total[0] + total[1]

    away = -(-(ghost_blocks + RIM) // 8) * 8

    def away_step(i, total):
        a = jnp.concatenate([spread(hi_right, i * GROUP + k, blocks, away, -1) for k in range(GROUP)], 1)
        b = jnp.concatenate([one_hot(lo_right, i * GROUP + k) for k in range(GROUP)], 1)
        return total + product(a, b)

    total = lax.fori_loop(0, rows // GROUP, away_step, jnp.zeros((5 * PIECES * away, BLK), jnp.float32))
    total = fold(total, away)
    for s in range(n_sub):
        gback_send[s] = total[:, s * capacity : (s + 1) * capacity, :]
    rback_send[...] = total[:, ghost_blocks : ghost_blocks + RIM, :]
    gback_copies = [
        pltpu.make_async_remote_copy(
            src_ref=gback_send.at[sub_peer(off)],
            dst_ref=gback_recv.at[off],
            send_sem=gback_send_sem.at[off],
            recv_sem=gback_recv_sem.at[off],
            device_id=(me_dom, sub_peer(off)),
            device_id_type=MESH,
        )
        for off in range(1, n_sub)
    ]
    for copy in gback_copies:
        copy.start()
    rback_copy = pltpu.make_async_remote_copy(
        src_ref=rback_send,
        dst_ref=rback_recv,
        send_sem=rback_send_sem,
        recv_sem=rback_recv_sem,
        device_id=(after, me_sub),
        device_id_type=MESH,
    )
    rback_copy.start()

    def local_step(i, total):
        a = [spread(hi_left, i * GROUP + k, 0, blocks, 1) for k in range(GROUP)]
        a += [spread(hi_right, i * GROUP + k, 0, blocks, -1) for k in range(GROUP)]
        b = [one_hot(lo_left, i * GROUP + k) for k in range(GROUP)]
        b += [one_hot(lo_right, i * GROUP + k) for k in range(GROUP)]
        return total + product(jnp.concatenate(a, 1), jnp.concatenate(b, 1))

    total = lax.fori_loop(0, rows // GROUP, local_step, jnp.zeros((5 * PIECES * blocks, BLK), jnp.float32))
    net = fold(total, blocks)

    for copy in dmin_copies:
        copy.wait()
    smallest = min_group[...]
    for off in range(1, n_dom):
        smallest = jnp.minimum(smallest, min_dom[off])
    time_step = courant * smallest
    step_out[...] = time_step
    time_step = time_step[0:1, :]

    rback_copy.wait()
    for copy in gback_copies:
        copy.wait()

    place = lax.broadcasted_iota(jnp.int32, (blocks, BLK), 0)
    density = jnp.exp(cells[0])
    pressure = jnp.exp(cells[4])
    square = cells[1] * cells[1] + cells[2] * cells[2] + cells[3] * cells[3]
    energy = pressure / (adiabatic - 1.0) + 0.5 * density * square
    conserved = [density, density * cells[1], density * cells[2], density * cells[3], energy]
    for c in range(5):
        sums = net[c]
        for h in range(RIM):
            sums = sums + jnp.where(place == h, rback_recv[c, h : h + 1, :], 0.0)
        for off in range(1, n_sub):
            sender = lax.rem(me_sub + n_sub - off, n_sub)
            for j in range(capacity):
                wanted = send_list[sender * capacity + j]
                sums = sums + jnp.where(place == wanted, gback_recv[off, c, j : j + 1, :], 0.0)
        rate = -sums / volume[...]
        rate_out[c] = rate
        new_out[c] = conserved[c] + time_step * rate


def body(mesh_sizes, *args):
    (primitive, gradient, volume, face_left, face_right, face_angles, face_area, face_offsets) = args[:8]
    (rim_left, rim_right, rim_angles, rim_area, rim_offsets, send_list) = args[8:]
    n_dom, n_sub = mesh_sizes
    cells = primitive.shape[1]
    blocks = cells // BLK
    face_rows = face_left.shape[0] // BLK
    capacity = send_list.shape[0] // n_sub
    padded = face_rows + 8
    dims = (n_dom, n_sub, capacity, blocks, face_rows)
    f32, i32 = jnp.float32, jnp.int32
    vmem = pl.BlockSpec(memory_space=pltpu.VMEM)
    smem = pl.BlockSpec(memory_space=pltpu.SMEM)
    sem = pltpu.SemaphoreType.DMA
    rate, new, step = pl.pallas_call(
        functools.partial(kernel, dims),
        out_shape=(
            jax.ShapeDtypeStruct((5, blocks, BLK), f32),
            jax.ShapeDtypeStruct((5, blocks, BLK), f32),
            jax.ShapeDtypeStruct((8, BLK), f32),
        ),
        in_specs=[smem] + [vmem] * 13,
        out_specs=(vmem, vmem, vmem),
        scratch_shapes=[
            pltpu.VMEM((n_sub, capacity, 24, BLK), f32),
            pltpu.VMEM((n_sub, capacity, 24, BLK), f32),
            pltpu.VMEM((RIM, 24, BLK), f32),
            pltpu.VMEM((blocks, 24, BLK), f32),
            pltpu.VMEM((8, BLK), f32),
            pltpu.VMEM((n_sub, 8, BLK), f32),
            pltpu.VMEM((8, BLK), f32),
            pltpu.VMEM((n_dom, 8, BLK), f32),
            pltpu.VMEM((n_sub, 5, capacity, BLK), f32),
            pltpu.VMEM((n_sub, 5, capacity, BLK), f32),
            pltpu.VMEM((5, RIM, BLK), f32),
            pltpu.VMEM((5, RIM, BLK), f32),
            pltpu.VMEM((5, blocks, BLK), f32),
            pltpu.VMEM((padded, BLK), i32),
            pltpu.VMEM((padded, BLK), i32),
            pltpu.VMEM((padded, BLK), i32),
            pltpu.VMEM((padded, BLK), i32),
            pltpu.VMEM((2, padded, BLK), f32),
            pltpu.VMEM((6, padded, BLK), f32),
            pltpu.VMEM((padded, BLK), f32),
            pltpu.VMEM((20, padded, BLK), f32),
            pltpu.VMEM((20, padded, BLK), f32),
            pltpu.VMEM((5 * PIECES, padded, BLK), f32),
            sem((n_sub,)),
            sem((n_sub,)),
            sem,
            sem,
            sem((n_sub,)),
            sem((n_sub,)),
            sem((n_dom,)),
            sem((n_dom,)),
            sem((n_sub,)),
            sem((n_sub,)),
            sem,
            sem,
        ],
        compiler_params=pltpu.CompilerParams(collective_id=0, has_side_effects=True),
        name="hydro_step",
    )(
        send_list,
        primitive,
        gradient,
        volume.reshape(blocks, BLK),
        face_left.reshape(face_rows, BLK),
        face_right.reshape(face_rows, BLK),
        face_angles,
        face_area.reshape(face_rows, BLK),
        face_offsets,
        rim_left.reshape(RIM, BLK),
        rim_right.reshape(RIM, BLK),
        rim_angles,
        rim_area.reshape(RIM, BLK),
        rim_offsets,
    )
    return rate.reshape(5, cells), new.reshape(5, cells), step[0, 0]


def solution(mesh):
    both = ("dom", "sub")
    wide, flat = P(None, both), P(both)
    in_specs = (wide, wide, flat, flat, flat, wide, flat, wide, flat, flat, wide, flat, wide, flat)
    out_specs = (wide, wide, P())
    step = functools.partial(body, (mesh.shape["dom"], mesh.shape["sub"]))
    return jax.shard_map(step, mesh=mesh, in_specs=in_specs, out_specs=out_specs, check_vma=False)
```

time: 220 us -> 38.2 us (0.17)
  other arithmetic: 92.7 us -> 0 us
  local copies, waits for them, and re-layouts: 67.3 us -> 2.66 us
  blocking collectives: 42.1 us -> 0 us
  Pallas kernels: 0 us -> 34.7 us
  starting transfers between devices: 14.2 us -> 0 us
  between operations: 3.26 us -> 0.65 us
    scatter-add x6 -> x0, other arithmetic: 77.9 us -> none  [the longest x2 68.2 us: body(): totals = jnp.zeros((5, combined.shape[1]), jnp.float32).at[:, face_left]....]
    gather x11 -> x0, local copies, waits for them, and re-layouts: 49.6 us -> none  [the longest x2 23.3 us: body(): jnp.take(packed, face_left, axis=1)]
    pmin x1 -> x0, blocking collectives: 42.1 us -> none  [body(): smallest = lax.pmin(local_limit, ('dom', 'sub'))]
    pallas_call x0 -> x1, Pallas kernels: none -> 34.7 us  [body(): pl.pallas_call(functools.partial(kernel, dims), out_shape=(jax.ShapeDtype...]
    all_to_all x2 -> x0, starting transfers between devices: 7.56 us -> none  [the longest x1 4.26 us: body(): lax.all_to_all(outgoing, 'sub', split_axis=1, concat_axis=1, tiled=True)]
    ppermute x2 -> x0, starting transfers between devices: 6.6 us -> none  [shifted(): lax.ppermute(value, axis, [(source, source + steps) for source in range(f...]
    unnamed x59 -> x0, local copies, waits for them, and re-layouts: 3.55 us -> none
    mul x4 -> x0, local copies, waits for them, and re-layouts: 3.19 us -> none  [the longest x1 2.22 us: body(): hllc_flux(jnp.take(packed, face_left, axis=1), jnp.take(combined, face_ri...]
  transfers between devices with their start and end apart: 4 -> 0, of which waited for: 0 -> 0; matrix products, arithmetic and copies ran while one was open for 69% -> 0% of each run, Pallas kernels for 0% -> 0%
where the time goes in v1:
time: 38.2 us; the launch traced here: 38 us
  Pallas kernels  34.7 us (91%)
  local copies, waits for them, and re-layouts  2.66 us (7%)
  between operations  0.65 us (2%)
    pallas_call x1, Pallas kernels, body(): pl.pallas_call(functools.partial(kernel, dims), out_shape=(jax.ShapeDtype...  34.7 us
    reshape x1, local copies, waits for them, and re-layouts, body(): return (rate.reshape(5, cells), new.reshape(5, cells), step[0, 0])  1.48 us
    slice x1, local copies, waits for them, and re-layouts, body(): return (rate.reshape(5, cells), new.reshape(5, cells), step[0, 0])  1.18 us

profile of v1, /device:TPU:0, one launch (start us, length us, event | category | flops | bytes accessed | tf_op | source)
XLA Modules:
  0.0 38.0 jit_solution(14009282555739361382)
XLA Ops:
  0.6 34.7 %hydro_step.1 = (f32[5,16,128]{2,1,0:T(8,128)}, f32[5,16,128]{2,1,0:T(8,128)}, f32[8,128]{1,0:T(8,128)}) custom-call(s32[16]{0:T(128)} %send_list.1, f32[5,2048]{1,0:T(8,128)} %prim.1, f32[15,2048]{1,0:T(8,128)} %grad.1, f32[16,128]{1,0:T(8,128)} %bitcast.19, s32[48,128]{1,0:T(8,128)} %bitcast.16, s32[48,128]{1,0:T(8,128)} %bitcast.17, ...), custom_call_target="tpu_custom_call" | custom-call | tf_op jit(solution)/shard_map/hydro_step/pallas_call | solution.py:458
  35.3 1.2 %slice.3 = f32[1,1]{1,0:T(1,128)} slice(f32[8,128]{1,0:T(8,128)} %get-tuple-element.8), slice={[0:1], [0:1]} | slice | bytes 8 | tf_op jit(solution)/shard_map/slice | solution.py:522
  36.5 1.5 %copy_bitcast_fusion = (f32[5,2048]{1,0:T(8,128)}, f32[5,2048]{1,0:T(8,128)}) fusion(f32[1,5,16,128]{3,2,1,0:T(8,128)} %bitcast.15, f32[1,5,16,128]{3,2,1,0:T(8,128)} %bitcast.14), kind=kLoop, calls=%fused_computation | loop fusion | bytes 163840 | tf_op jit(solution)/shard_map/reshape | solution.py:522

commit v2 on v1

--- a/solution.py
+++ b/solution.py
@@ -8,7 +8,7 @@
 
 BLK = 128
 RIM = 4
-GROUP = 4
+GROUP = 13
 PIECES = 2
 
 adiabatic = 5.0 / 3.0
@@ -77,9 +77,17 @@
     return jnp.take_along_axis(table, index, axis=1, mode="promise_in_bounds")
 
 
-def kernel(
+def kernel(dims, send_list, *refs):
+    staged = refs[16:29]
+    stage_sem = refs[29]
+    loads = [pltpu.make_async_copy(source, staged[k], stage_sem.at[k]) for k, source in enumerate(refs[:13])]
+    step(dims, send_list, loads, *staged, *refs[13:16], *refs[30:])
+
+
+def step(
     dims,
     send_list,
+    loads,
     prim,
     grad,
     volume,
@@ -134,6 +142,7 @@
 ):
     n_dom, n_sub, capacity, blocks, face_rows = dims
     rows = face_rows + RIM
+    group = max(k for k in range(1, GROUP + 1) if rows % k == 0)
     ghost_blocks = n_sub * capacity
     me_dom = lax.axis_index("dom")
     me_sub = lax.axis_index("sub")
@@ -152,6 +161,11 @@
     for off in range(1, n_dom):
         pl.semaphore_signal(barrier, inc=1, device_id=(dom_peer(off), me_sub), device_id_type=MESH)
 
+    for load in loads:
+        load.start()
+    for k in (0, 1):
+        loads[k].wait()
+
     for h in range(blocks):
         table[h, 0:5, :] = prim[:, h * BLK : (h + 1) * BLK]
         table[h, 5:8, :] = jnp.zeros((3, BLK), jnp.float32)
@@ -162,6 +176,9 @@
         for j in range(capacity):
             block = jnp.maximum(send_list[sub_peer(off) * capacity + j], 0)
             outgoing[off, j] = table[block]
+
+    for k in range(2, len(loads)):
+        loads[k].wait()
 
     for r in range(5):
         for h in range(blocks):
@@ -173,6 +190,61 @@
     limit = jnp.exp(jnp.log(volume[...]) * (1.0 / 3.0)) / signal
     local_min = jnp.min(limit)
     min_own[...] = jnp.full(min_own.shape, local_min, jnp.float32)
+
+    hi_left[0:face_rows, :] = face_left[...] // BLK
+    lo_left[0:face_rows, :] = lax.rem(face_left[...], BLK)
+    hi_right[0:face_rows, :] = face_right[...] // BLK
+    lo_right[0:face_rows, :] = lax.rem(face_right[...], BLK)
+    area[0:face_rows, :] = face_area[...]
+    twice = lambda ref: jnp.concatenate([ref[...], ref[...]], 0)
+    hi_left[face_rows : face_rows + 8, :] = twice(rim_left) // BLK + (blocks - RIM)
+    lo_left[face_rows : face_rows + 8, :] = lax.rem(twice(rim_left), BLK)
+    hi_right[face_rows : face_rows + 8, :] = twice(rim_right) // BLK + (blocks + ghost_blocks)
+    lo_right[face_rows : face_rows + 8, :] = lax.rem(twice(rim_right), BLK)
+    last = me_dom == n_dom - 1
+    area[face_rows : face_rows + 8, :] = twice(rim_area)
+    for s in range(face_rows):
+        for r in range(2):
+            angles[r, s : s + 1, :] = face_angles[r : r + 1, s * BLK : (s + 1) * BLK]
+        for r in range(6):
+            offsets[r, s : s + 1, :] = face_offsets[r : r + 1, s * BLK : (s + 1) * BLK]
+    for s in range(8):
+        t = s % RIM
+        for r in range(2):
+            angles[r, face_rows + s : face_rows + s + 1, :] = rim_angles[r : r + 1, t * BLK : (t + 1) * BLK]
+        for r in range(6):
+            offsets[r, face_rows + s : face_rows + s + 1, :] = rim_offsets[r : r + 1, t * BLK : (t + 1) * BLK]
+
+    tail = pl.ds(face_rows, 8)
+
+    fields = list(range(5)) + list(range(8, 23))
+
+    def gather(hi, lo, entries, names, start):
+        match = [hi == name for name in names]
+        out = []
+        for c, place in enumerate(fields):
+            value = start(c)
+            for entry, hit in zip(entries, match):
+                row = entry[place : place + 1, :]
+                value = jnp.where(hit, lane_gather(row, lo), value)
+            out.append(value)
+        return out
+
+    def gather_into(target, hi, lo, here, entries, names, keep):
+        start = (lambda c: target[c, here, :]) if keep else (lambda c: jnp.zeros((8, BLK), jnp.float32))
+        for c, value in enumerate(gather(hi[here, :], lo[here, :], entries, names, start)):
+            target[c, here, :] = value
+
+    def gather_main(target, hi, lo, entries, names, keep):
+        def one(g, carry):
+            here = pl.ds(pl.multiple_of(g * 8, 8), 8)
+            gather_into(target, hi, lo, here, entries, names, keep)
+            return carry
+
+        lax.fori_loop(0, face_rows // 8, one, 0)
+
+    own = [table.at[h] for h in range(blocks)]
+    gather_main(gathered_l, hi_left, lo_left, own, range(blocks), False)
 
     pl.semaphore_wait(barrier, n_sub - 1 + n_dom - 1)
 
@@ -214,56 +286,8 @@
     for copy in min_copies:
         copy.start()
 
-    hi_left[0:face_rows, :] = face_left[...] // BLK
-    lo_left[0:face_rows, :] = lax.rem(face_left[...], BLK)
-    hi_right[0:face_rows, :] = face_right[...] // BLK
-    lo_right[0:face_rows, :] = lax.rem(face_right[...], BLK)
-    area[0:face_rows, :] = face_area[...]
-    twice = lambda ref: jnp.concatenate([ref[...], ref[...]], 0)
-    hi_left[face_rows : face_rows + 8, :] = twice(rim_left) // BLK + (blocks - RIM)
-    lo_left[face_rows : face_rows + 8, :] = lax.rem(twice(rim_left), BLK)
-    hi_right[face_rows : face_rows + 8, :] = twice(rim_right) // BLK + (blocks + ghost_blocks)
-    lo_right[face_rows : face_rows + 8, :] = lax.rem(twice(rim_right), BLK)
-    last = me_dom == n_dom - 1
-    area[face_rows : face_rows + 8, :] = twice(rim_area)
-    for s in range(face_rows):
-        for r in range(2):
-            angles[r, s : s + 1, :] = face_angles[r : r + 1, s * BLK : (s + 1) * BLK]
-        for r in range(6):
-            offsets[r, s : s + 1, :] = face_offsets[r : r + 1, s * BLK : (s + 1) * BLK]
-    for s in range(8):
-        t = s % RIM
-        for r in range(2):
-            angles[r, face_rows + s : face_rows + s + 1, :] = rim_angles[r : r + 1, t * BLK : (t + 1) * BLK]
-        for r in range(6):
-            offsets[r, face_rows + s : face_rows + s + 1, :] = rim_offsets[r : r + 1, t * BLK : (t + 1) * BLK]
-
-    main = pl.ds(0, face_rows)
-    tail = pl.ds(face_rows, 8)
-
-    def gather_local(count, place, shift):
-        def step(r, carry):
-            hl, ll, hr, lr = (ref[main, :] for ref in (hi_left, lo_left, hi_right, lo_right))
-            left = jnp.zeros(hl.shape, jnp.float32)
-            right = jnp.zeros(hl.shape, jnp.float32)
-            for h in range(blocks):
-                row = table[h, pl.ds(r + place, 1), :]
-                left = jnp.where(hl == h, lane_gather(row, ll), left)
-                right = jnp.where(hr == h, lane_gather(row, lr), right)
-            gathered_l[r + shift, main, :] = left
-            gathered_r[r + shift, main, :] = right
-            hl, ll = hi_left[tail, :], lo_left[tail, :]
-            left = jnp.zeros(hl.shape, jnp.float32)
-            for h in range(blocks - RIM, blocks):
-                row = table[h, pl.ds(r + place, 1), :]
-                left = jnp.where(hl == h, lane_gather(row, ll), left)
-            gathered_l[r + shift, tail, :] = left
-            return carry
-
-        lax.fori_loop(0, count, step, 0)
-
-    gather_local(5, 0, 0)
-    gather_local(15, 8, 5)
+    gather_into(gathered_l, hi_left, lo_left, tail, own[blocks - RIM :], range(blocks - RIM, blocks), False)
+    gather_main(gathered_r, hi_right, lo_right, own, range(blocks), False)
 
     for copy in min_copies:
         copy.wait()
@@ -274,20 +298,9 @@
 
     rim_copy.wait()
 
-    def gather_rim(count, place, shift):
-        def step(r, carry):
-            hr, lr = hi_right[tail, :], lo_right[tail, :]
-            right = jnp.zeros(hr.shape, jnp.float32)
-            for h in range(RIM):
-                row = following[h, pl.ds(r + place, 1), :]
-                right = jnp.where(hr == h + blocks + ghost_blocks, lane_gather(row, lr), right)
-            gathered_r[r + shift, tail, :] = right
-            return carry
-
-        lax.fori_loop(0, count, step, 0)
-
-    gather_rim(5, 0, 0)
-    gather_rim(15, 8, 5)
+    first = blocks + ghost_blocks
+    nexts = [following.at[h] for h in range(RIM)]
+    gather_into(gathered_r, hi_right, lo_right, tail, nexts, range(first, first + RIM), False)
 
     dmin_copies = [
         pltpu.make_async_remote_copy(
@@ -306,22 +319,13 @@
     for copy in ghost_copies:
         copy.wait()
 
-    def gather_ghosts(count, place, shift):
-        def step(r, carry):
-            hr, lr = hi_right[main, :], lo_right[main, :]
-            right = gathered_r[r + shift, main, :]
-            for off in range(1, n_sub):
-                sender = lax.rem(me_sub + n_sub - off, n_sub)
-                for j in range(capacity):
-                    row = ghosts[off, j, pl.ds(r + place, 1), :]
-                    right = jnp.where(hr == blocks + sender * capacity + j, lane_gather(row, lr), right)
-            gathered_r[r + shift, main, :] = right
-            return carry
-
-        lax.fori_loop(0, count, step, 0)
-
-    gather_ghosts(5, 0, 0)
-    gather_ghosts(15, 8, 5)
+    entries, names = [], []
+    for off in range(1, n_sub):
+        sender = lax.rem(me_sub + n_sub - off, n_sub)
+        for j in range(capacity):
+            entries.append(ghosts.at[off, j])
+            names.append(blocks + sender * capacity + j)
+    gather_main(gathered_r, hi_right, lo_right, entries, names, True)
 
     def flux_step(g, carry):
         here = pl.ds(pl.multiple_of(g * 8, 8), 8)
@@ -366,11 +370,11 @@
     away = -(-(ghost_blocks + RIM) // 8) * 8
 
     def away_step(i, total):
-        a = jnp.concatenate([spread(hi_right, i * GROUP + k, blocks, away, -1) for k in range(GROUP)], 1)
-        b = jnp.concatenate([one_hot(lo_right, i * GROUP + k) for k in range(GROUP)], 1)
+        a = jnp.concatenate([spread(hi_right, i * group + k, blocks, away, -1) for k in range(group)], 1)
+        b = jnp.concatenate([one_hot(lo_right, i * group + k) for k in range(group)], 1)
         return total + product(a, b)
 
-    total = lax.fori_loop(0, rows // GROUP, away_step, jnp.zeros((5 * PIECES * away, BLK), jnp.float32))
+    total = lax.fori_loop(0, rows // group, away_step, jnp.zeros((5 * PIECES * away, BLK), jnp.float32))
     total = fold(total, away)
     for s in range(n_sub):
         gback_send[s] = total[:, s * capacity : (s + 1) * capacity, :]
@@ -399,13 +403,13 @@
     rback_copy.start()
 
     def local_step(i, total):
-        a = [spread(hi_left, i * GROUP + k, 0, blocks, 1) for k in range(GROUP)]
-        a += [spread(hi_right, i * GROUP + k, 0, blocks, -1) for k in range(GROUP)]
-        b = [one_hot(lo_left, i * GROUP + k) for k in range(GROUP)]
-        b += [one_hot(lo_right, i * GROUP + k) for k in range(GROUP)]
+        a = [spread(hi_left, i * group + k, 0, blocks, 1) for k in range(group)]
+        a += [spread(hi_right, i * group + k, 0, blocks, -1) for k in range(group)]
+        b = [one_hot(lo_left, i * group + k) for k in range(group)]
+        b += [one_hot(lo_right, i * group + k) for k in range(group)]
         return total + product(jnp.concatenate(a, 1), jnp.concatenate(b, 1))
 
-    total = lax.fori_loop(0, rows // GROUP, local_step, jnp.zeros((5 * PIECES * blocks, BLK), jnp.float32))
+    total = lax.fori_loop(0, rows // group, local_step, jnp.zeros((5 * PIECES * blocks, BLK), jnp.float32))
     net = fold(total, blocks)
 
     for copy in dmin_copies:
@@ -414,7 +418,7 @@
     for off in range(1, n_dom):
         smallest = jnp.minimum(smallest, min_dom[off])
     time_step = courant * smallest
-    step_out[...] = time_step
+    step_out[0] = jnp.min(time_step)
     time_step = time_step[0:1, :]
 
     rback_copy.wait()
@@ -455,16 +459,33 @@
     vmem = pl.BlockSpec(memory_space=pltpu.VMEM)
     smem = pl.BlockSpec(memory_space=pltpu.SMEM)
     sem = pltpu.SemaphoreType.DMA
+    operands = (
+        primitive,
+        gradient,
+        volume.reshape(blocks, BLK),
+        face_left.reshape(face_rows, BLK),
+        face_right.reshape(face_rows, BLK),
+        face_angles,
+        face_area.reshape(face_rows, BLK),
+        face_offsets,
+        rim_left.reshape(RIM, BLK),
+        rim_right.reshape(RIM, BLK),
+        rim_angles,
+        rim_area.reshape(RIM, BLK),
+        rim_offsets,
+    )
     rate, new, step = pl.pallas_call(
         functools.partial(kernel, dims),
         out_shape=(
             jax.ShapeDtypeStruct((5, blocks, BLK), f32),
             jax.ShapeDtypeStruct((5, blocks, BLK), f32),
-            jax.ShapeDtypeStruct((8, BLK), f32),
+            jax.ShapeDtypeStruct((1,), f32),
         ),
-        in_specs=[smem] + [vmem] * 13,
-        out_specs=(vmem, vmem, vmem),
-        scratch_shapes=[
+        in_specs=[smem] + [pl.BlockSpec(memory_space=pl.ANY)] * 13,
+        out_specs=(vmem, vmem, smem),
+        scratch_shapes=[pltpu.VMEM(x.shape, x.dtype) for x in operands]
+        + [
+            sem((len(operands),)),
             pltpu.VMEM((n_sub, capacity, 24, BLK), f32),
             pltpu.VMEM((n_sub, capacity, 24, BLK), f32),
             pltpu.VMEM((RIM, 24, BLK), f32),
@@ -505,21 +526,9 @@
         name="hydro_step",
     )(
         send_list,
-        primitive,
-        gradient,
-        volume.reshape(blocks, BLK),
-        face_left.reshape(face_rows, BLK),
-        face_right.reshape(face_rows, BLK),
-        face_angles,
-        face_area.reshape(face_rows, BLK),
-        face_offsets,
-        rim_left.reshape(RIM, BLK),
-        rim_right.reshape(RIM, BLK),
-        rim_angles,
-        rim_area.reshape(RIM, BLK),
-        rim_offsets,
+        *operands,
     )
-    return rate.reshape(5, cells), new.reshape(5, cells), step[0, 0]
+    return rate.reshape(5, cells), new.reshape(5, cells), step.reshape(())
 
 
 def solution(mesh):

time: 38.2 us -> 26.4 us (0.69)
  Pallas kernels: 34.7 us -> 22.4 us
  between operations: 0.65 us -> 2.33 us
  local copies, waits for them, and re-layouts: 2.66 us -> 1.48 us
    pallas_call x1, Pallas kernels: 34.7 us -> 22.4 us  [body(): pl.pallas_call(functools.partial(kernel, dims), out_shape=(jax.ShapeDtype...]
    slice x1 -> x0, local copies, waits for them, and re-layouts: 1.18 us -> none  [body(): return (rate.reshape(5, cells), new.reshape(5, cells), step[0, 0])]
where the time goes in v2:
time: 26.4 us; the launch traced here: 26.2 us
  Pallas kernels  22.4 us (85%)
  between operations  2.33 us (9%)
  local copies, waits for them, and re-layouts  1.48 us (6%)
    pallas_call x1, Pallas kernels, body(): pl.pallas_call(functools.partial(kernel, dims), out_shape=(jax.ShapeDtype...  22.4 us
    reshape x1, local copies, waits for them, and re-layouts, body(): return (rate.reshape(5, cells), new.reshape(5, cells), step.reshape(()))  1.48 us

profile of v2, /device:TPU:0, one launch (start us, length us, event | category | flops | bytes accessed | tf_op | source)
XLA Modules:
  0.0 26.2 jit_solution(5494996939188719743)
XLA Ops:
  0.6 22.4 %hydro_step.1 = (f32[5,16,128]{2,1,0:T(8,128)}, f32[5,16,128]{2,1,0:T(8,128)}, f32[1]{0:T(128)}) custom-call(s32[16]{0:T(128)} %send_list.1, f32[5,2048]{1,0:T(8,128)} %refs_0_.1, f32[15,2048]{1,0:T(8,128)} %refs_1_.1, f32[16,128]{1,0:T(8,128)} %bitcast.19, s32[48,128]{1,0:T(8,128)} %bitcast.16, s32[48,128]{1,0:T(8,128)} %bitcast.17, f32[2,6144]{1,0:T(2,128)} %refs_5_.1, ...), custom_call_target="tpu_custom_call" | custom-call | tf_op jit(solution)/shard_map/hydro_step/pallas_call | solution.py:477
  23.0 1.5 %copy_bitcast_fusion = (f32[5,2048]{1,0:T(8,128)}, f32[5,2048]{1,0:T(8,128)}) fusion(f32[1,5,16,128]{3,2,1,0:T(8,128)} %bitcast.15, f32[1,5,16,128]{3,2,1,0:T(8,128)} %bitcast.14), kind=kLoop, calls=%fused_computation | loop fusion | bytes 163840 | tf_op jit(solution)/shard_map/reshape | solution.py:531

commit v3 on v2

--- a/solution.py
+++ b/solution.py
@@ -235,16 +235,17 @@
         for c, value in enumerate(gather(hi[here, :], lo[here, :], entries, names, start)):
             target[c, here, :] = value
 
-    def gather_main(target, hi, lo, entries, names, keep):
+    def gather_main(target, hi, lo, entries, names, keep, low=0, high=face_rows // 8):
         def one(g, carry):
             here = pl.ds(pl.multiple_of(g * 8, 8), 8)
             gather_into(target, hi, lo, here, entries, names, keep)
             return carry
 
-        lax.fori_loop(0, face_rows // 8, one, 0)
+        lax.fori_loop(low, high, one, 0)
 
     own = [table.at[h] for h in range(blocks)]
     gather_main(gathered_l, hi_left, lo_left, own, range(blocks), False)
+    gather_main(gathered_r, hi_right, lo_right, own, range(blocks), False, 0, 1)
 
     pl.semaphore_wait(barrier, n_sub - 1 + n_dom - 1)
 
@@ -287,7 +288,7 @@
         copy.start()
 
     gather_into(gathered_l, hi_left, lo_left, tail, own[blocks - RIM :], range(blocks - RIM, blocks), False)
-    gather_main(gathered_r, hi_right, lo_right, own, range(blocks), False)
+    gather_main(gathered_r, hi_right, lo_right, own, range(blocks), False, 1)
 
     for copy in min_copies:
         copy.wait()
@@ -343,7 +344,7 @@
             pieces[5 + c, here, :] = value - big
         return carry
 
-    lax.fori_loop(0, (face_rows + 8) // 8, flux_step, 0)
+    lax.fori_loop(0, (face_rows + 8) // 8, flux_step, 0, unroll=True)
 
     lane_iota = lax.broadcasted_iota(jnp.int32, (BLK, BLK), 0)
 

time: 26.4 us -> 26.7 us (1.011)
  no operation moved by 1% of the time
where the time goes in v3:
time: 26.7 us; the launch traced here: 26.4 us
  Pallas kernels  22.6 us (85%)
  between operations  2.33 us (9%)
  local copies, waits for them, and re-layouts  1.48 us (6%)
    pallas_call x1, Pallas kernels, body(): pl.pallas_call(functools.partial(kernel, dims), out_shape=(jax.ShapeDtype...  22.6 us
    reshape x1, local copies, waits for them, and re-layouts, body(): return (rate.reshape(5, cells), new.reshape(5, cells), step.reshape(()))  1.48 us

profile of v3, /device:TPU:0, one launch (start us, length us, event | category | flops | bytes accessed | tf_op | source)
XLA Modules:
  0.0 26.4 jit_solution(10676352676378331383)
XLA Ops:
  0.6 22.6 %hydro_step.1 = (f32[5,16,128]{2,1,0:T(8,128)}, f32[5,16,128]{2,1,0:T(8,128)}, f32[1]{0:T(128)}) custom-call(s32[16]{0:T(128)} %send_list.1, f32[5,2048]{1,0:T(8,128)} %refs_0_.1, f32[15,2048]{1,0:T(8,128)} %refs_1_.1, f32[16,128]{1,0:T(8,128)} %bitcast.19, s32[48,128]{1,0:T(8,128)} %bitcast.16, s32[48,128]{1,0:T(8,128)} %bitcast.17, f32[2,6144]{1,0:T(2,128)} %refs_5_.1, ...), custom_call_target="tpu_custom_call" | custom-call | tf_op jit(solution)/shard_map/hydro_step/pallas_call | solution.py:478
  23.3 1.5 %copy_bitcast_fusion = (f32[5,2048]{1,0:T(8,128)}, f32[5,2048]{1,0:T(8,128)}) fusion(f32[1,5,16,128]{3,2,1,0:T(8,128)} %bitcast.15, f32[1,5,16,128]{3,2,1,0:T(8,128)} %bitcast.14), kind=kLoop, calls=%fused_computation | loop fusion | bytes 163840 | tf_op jit(solution)/shard_map/reshape | solution.py:532
